TPU v7x, 32 devices: a whole 2x2x4 slice. The times are simulated.
32 devices in a mesh: fsdp: 8 (over z, x), grp: 4 (over y, core).
Axes of the slice: x: 2, y: 2, z: 4, core: 2. Of those that a mesh axis runs over, the one named last changes fastest.
Arguments:
- grad: bfloat16 [28672, 8192], P('fsdp', 'grp'), may hold values from -6 to 6
- projector_t: bfloat16 [1024, 8192], P('fsdp', 'grp'), may hold values from -0.0625 to 0.0625
- first_moment: float32 [28672, 1024], P('fsdp', 'grp'), may hold values from -3 to 3
- second_moment: float32 [28672, 1024], P('fsdp', 'grp'), may hold values from 0.0001 to 0.01
Outputs:
- update: float32 [28672, 8192], P('fsdp', 'grp')
- first_new: float32 [28672, 1024], P('fsdp', 'grp')
- second_new: float32 [28672, 1024], P('fsdp', 'grp')
All inputs are finite; a program needn't handle non-finite values.
Results may differ from a plain program's by a relative error of at most 0.0029.
Values may be sent and summed in bfloat16 or wider, within the bound.
A program may use at most 128 MiB of HBM per device.

v0:
```python
import jax
import jax.numpy as jnp
from jax import lax
from jax.sharding import PartitionSpec as P

STEP = 10


def body(grad, projector_t, first_moment, second_moment):
    whole = lax.all_gather(projector_t, "fsdp", axis=0, tiled=True)
    partial_value = lax.dot_general(
        grad, whole, (((1,), (1,)), ((), ())), preferred_element_type=jnp.float32
    )
    projected = lax.psum_scatter(partial_value, "grp", scatter_dimension=1, tiled=True)
    first_new = 0.9 * first_moment + 0.1 * projected
    second_new = 0.999 * second_moment + 0.001 * projected * projected
    correct_one = 1.0 - 0.9**STEP
    correct_two = 1.0 - 0.999**STEP
    normalized = (first_new / correct_one / (jnp.sqrt(second_new / correct_two) + 1e-08)).astype(
        jnp.bfloat16
    )
    full_step = lax.all_gather(normalized, "grp", axis=1, tiled=True)
    update = jnp.dot(full_step, whole, preferred_element_type=jnp.float32)
    return (update, first_new, second_new)


def solution(mesh):
    return jax.shard_map(
        body,
        mesh=mesh,
        in_specs=(P("fsdp", "grp"), P("fsdp", "grp"), P("fsdp", "grp"), P("fsdp", "grp")),
        out_specs=(P("fsdp", "grp"), P("fsdp", "grp"), P("fsdp", "grp")),
        check_vma=False,
    )
```

profile of v0, /device:TPU:0, one launch (start us, length us, event | category | flops | bytes accessed | tf_op | source)
XLA Modules:
  0.0 306.6 jit_solution(5147989194662069620)
XLA Ops:
  7.2 0.0 all-gather.3.cloned.1.call-start
  7.2 0.7 all-gather.3.cloned.1.call-update
  7.9 0.0 reduce-scatter.2.cloned.1.call-start
  7.9 77.7 %all-gather.3.cloned.1.call-done = bf16[1024,2048]{1,0:T(8,128)(2,1)} async-done(((bf16[128,2048]{1,0:T(8,128)(2,1)}), bf16[1024,2048]{1,0:T(8,128)(2,1)}) %all-gather.3.cloned.1.call-update) | async-done | bytes 4194320 | tf_op jit(solution)/shard_map/all_gather | solution.py:10
  85.6 21.8 %fusion.2 = f32[3584,1024]{1,0:T(8,128)} fusion(bf16[3584,2048]{1,0:T(8,128)(2,1)} %param.4, bf16[1024,2048]{1,0:T(8,128)(2,1)} %all-gather.3.cloned.1.call-done), kind=kOutput, calls=%fused_computation.4 | convolution fusion | flops 15032385536 | bytes 33554432 | tf_op jit(solution)/shard_map/dot_general | solution.py:11
  107.5 0.0 reduce-scatter.2.cloned.1.call-update
  107.5 0.0 all-gather.5.cloned.1.call-start
  107.6 108.7 %reduce-scatter.2.cloned.1.call-done = f32[3584,256]{1,0:T(8,128)} async-done(((f32[3584,1024]{1,0:T(8,128)}), f32[3584,256]{1,0:T(8,128)}) %reduce-scatter.2.cloned.1.call-update) | async-done | bytes 3670032 | tf_op jit(solution)/shard_map/reduce_scatter | solution.py:14
  216.3 7.7 %divide_convert_fusion = (bf16[3584,256]{1,0:T(8,128)(2,1)}, f32[3584,256]{1,0:T(8,128)}, f32[3584,256]{1,0:T(8,128)}) fusion(f32[3584,256]{1,0:T(8,128)} %reduce-scatter.2.cloned.1.call-done, f32[3584,256]{1,0:T(8,128)} %param.6, f32[3584,256]{1,0:T(8,128)} %param.7), kind=kLoop, calls=%fused_computation.2 | loop fusion | flops 11010048 | bytes 20185088 | tf_op jit(solution)/shard_map/convert_element_type | solution.py:19
  224.0 0.0 all-gather.5.cloned.1.call-update
  224.0 53.4 %all-gather.5.cloned.1.call-done = bf16[3584,1024]{1,0:T(8,128)(2,1)} async-done(((bf16[3584,256]{1,0:T(8,128)(2,1)}), bf16[3584,1024]{1,0:T(8,128)(2,1)}) %all-gather.5.cloned.1.call-update) | async-done | bytes 7340048 | tf_op jit(solution)/shard_map/all_gather | solution.py:22
  277.5 22.6 %fusion.3 = f32[3584,2048]{1,0:T(8,128)} fusion(bf16[3584,1024]{1,0:T(8,128)(2,1)} %all-gather.5.cloned.1.call-done, bf16[1024,2048]{1,0:T(8,128)(2,1)} %all-gather.3.cloned.1.call-done), kind=kOutput, calls=%fused_computation.5 | convolution fusion | flops 15032385536 | bytes 40894464 | tf_op jit(solution)/shard_map/dot_general | solution.py:23
Async XLA Ops:
  7.2 78.5 %all-gather.3.cloned.1.call-start = ((), (), s32[]{:S(2)}) async-start(), calls=%async_computation.1 | async-start | bytes 4718592 | tf_op jit(solution)/shard_map/all_gather | solution.py:10
  7.9 208.4 %reduce-scatter.2.cloned.1.call-start = ((), (), s32[]{:S(2)}) async-start(), calls=%async_computation.2 | async-start | bytes 18350080 | tf_op jit(solution)/shard_map/reduce_scatter | solution.py:14
  107.5 170.0 %all-gather.5.cloned.1.call-start = ((), (), s32[]{:S(2)}) async-start(), calls=%async_computation.3 | async-start | bytes 9175040 | tf_op jit(solution)/shard_map/all_gather | solution.py:22
Sparse Core Ops, SparseCore 0:
  10.1 75.4 all-gather.2
  107.6 108.6 reduce-scatter.1
  224.2 53.2 all-gather.4
where the time goes:
time: 307 us
  waiting for transfers between devices  241 us (79%)
  matrix products  44.4 us (14%)
  between operations  13.7 us (4%)
  other arithmetic  7.72 us (3%)
    reduce_scatter x1, waiting for transfers between devices, body(): lax.psum_scatter(partial_value, 'grp', scatter_dimension=1, tiled=True)  109 us
    all_gather x1, waiting for transfers between devices, body(): whole = lax.all_gather(projector_t, 'fsdp', axis=0, tiled=True)  77.7 us
    all_gather x1, waiting for transfers between devices, body(): full_step = lax.all_gather(normalized, 'grp', axis=1, tiled=True)  53.4 us
    dot_general x1, matrix products, body(): update = jnp.dot(full_step, whole, preferred_element_type=jnp.float32)  22.6 us
    dot_general x1, matrix products, body(): lax.dot_general(grad, whole, (((1,), (1,)), ((), ())), preferred_element_...  21.8 us
    convert_element_type x1, other arithmetic, body(): (first_new / correct_one / (jnp.sqrt(second_new / correct_two) + 1e-08))....  7.72 us
  transfers between devices with their start and end apart: 3, of which 3 were waited for; matrix products, arithmetic and copies ran while one was open for 0% of the time, Pallas kernels for 0%

commit v1 on v0

--- a/solution.py
+++ b/solution.py
@@ -19,7 +19,7 @@
     normalized = (first_new / correct_one / (jnp.sqrt(second_new / correct_two) + 1e-08)).astype(
         jnp.bfloat16
     )
-    full_step = lax.all_gather(normalized, "grp", axis=1, tiled=True)
+    full_step = jnp.concatenate(lax.all_gather(normalized, "grp"), axis=1)
     update = jnp.dot(full_step, whole, preferred_element_type=jnp.float32)
     return (update, first_new, second_new)
 

time: 307 us -> 318 us (1.036)
  local copies, waits for them, and re-layouts: 0 us -> 10.1 us
    all_gather x0 -> x1, local copies, waits for them, and re-layouts: none -> 10.1 us  [body(): full_step = jnp.concatenate(lax.all_gather(normalized, 'grp'), axis=1)]
where the time goes in v1:
time: 318 us
  waiting for transfers between devices  239 us (75%)
  matrix products  46.3 us (15%)
  between operations  13.7 us (4%)
  local copies, waits for them, and re-layouts  10.1 us (3%)
  other arithmetic  7.72 us (2%)
    reduce_scatter x1, waiting for transfers between devices, body(): lax.psum_scatter(partial_value, 'grp', scatter_dimension=1, tiled=True)  109 us
    all_gather x1, waiting for transfers between devices, body(): whole = lax.all_gather(projector_t, 'fsdp', axis=0, tiled=True)  77.7 us
    all_gather x1, waiting for transfers between devices, body(): full_step = jnp.concatenate(lax.all_gather(normalized, 'grp'), axis=1)  52.5 us
    dot_general x1, matrix products, body(): update = jnp.dot(full_step, whole, preferred_element_type=jnp.float32)  24.5 us
    dot_general x1, matrix products, body(): lax.dot_general(grad, whole, (((1,), (1,)), ((), ())), preferred_element_...  21.8 us
    all_gather x1, local copies, waits for them, and re-layouts, body(): full_step = jnp.concatenate(lax.all_gather(normalized, 'grp'), axis=1)  10.1 us
    convert_element_type x1, other arithmetic, body(): (first_new / correct_one / (jnp.sqrt(second_new / correct_two) + 1e-08))....  7.72 us
  transfers between devices with their start and end apart: 3, of which 3 were waited for; matrix products, arithmetic and copies ran while one was open for 0% of the time, Pallas kernels for 0%

profile of v1, /device:TPU:0, one launch (start us, length us, event | category | flops | bytes accessed | tf_op | source)
XLA Modules:
  0.0 317.6 jit_solution(4256818274934709007)
XLA Ops:
  7.2 0.0 all-gather.4.cloned.1.call-start
  7.2 0.7 all-gather.4.cloned.1.call-update
  7.9 0.0 reduce-scatter.2.cloned.1.call-start
  7.9 77.7 %all-gather.4.cloned.1.call-done = bf16[1024,2048]{1,0:T(8,128)(2,1)} async-done(((bf16[128,2048]{1,0:T(8,128)(2,1)}), bf16[1024,2048]{1,0:T(8,128)(2,1)}) %all-gather.4.cloned.1.call-update) | async-done | bytes 4194320 | tf_op jit(solution)/shard_map/all_gather | solution.py:10
  85.6 21.8 %fusion.2 = f32[3584,1024]{1,0:T(8,128)} fusion(bf16[3584,2048]{1,0:T(8,128)(2,1)} %param.4, bf16[1024,2048]{1,0:T(8,128)(2,1)} %all-gather.4.cloned.1.call-done), kind=kOutput, calls=%fused_computation.4 | convolution fusion | flops 15032385536 | bytes 33554432 | tf_op jit(solution)/shard_map/dot_general | solution.py:11
  107.5 0.0 reduce-scatter.2.cloned.1.call-update
  107.5 0.2 all-gather.6.cloned.1.call-start
  107.7 108.5 %reduce-scatter.2.cloned.1.call-done = f32[3584,256]{1,0:T(8,128)} async-done(((f32[3584,1024]{1,0:T(8,128)}), f32[3584,256]{1,0:T(8,128)}) %reduce-scatter.2.cloned.1.call-update) | async-done | bytes 3670032 | tf_op jit(solution)/shard_map/reduce_scatter | solution.py:14
  216.3 7.7 %divide_convert_fusion = (bf16[3584,256]{1,0:T(8,128)(2,1)}, f32[3584,256]{1,0:T(8,128)}, f32[3584,256]{1,0:T(8,128)}) fusion(f32[3584,256]{1,0:T(8,128)} %reduce-scatter.2.cloned.1.call-done, f32[3584,256]{1,0:T(8,128)} %param.6, f32[3584,256]{1,0:T(8,128)} %param.7), kind=kLoop, calls=%fused_computation.2 | loop fusion | flops 11010048 | bytes 20185088 | tf_op jit(solution)/shard_map/convert_element_type | solution.py:19
  224.0 0.0 all-gather.6.cloned.1.call-update
  224.0 52.5 %all-gather.6.cloned.1.call-done = bf16[14336,256]{1,0:T(8,128)(2,1)} async-done(((bf16[3584,256]{1,0:T(8,128)(2,1)}), bf16[14336,256]{1,0:T(8,128)(2,1)}) %all-gather.6.cloned.1.call-update) | async-done | bytes 7340048 | tf_op jit(solution)/shard_map/all_gather | solution.py:22
  276.5 10.1 %copy.7 = bf16[4,3584,256]{1,2,0:T(8,128)(2,1)} copy(bf16[4,3584,256]{2,1,0:T(8,128)(2,1)} %bitcast.8) | data formatting | bytes 14680064 | tf_op jit(solution)/shard_map/all_gather | solution.py:22
  286.6 24.5 %fusion.3 = f32[3584,2048]{1,0:T(8,128)} fusion(bf16[3584,1024]{0,1:T(8,128)(2,1)} %bitcast.9, bf16[1024,2048]{1,0:T(8,128)(2,1)} %all-gather.4.cloned.1.call-done), kind=kOutput, calls=%fused_computation.5 | convolution fusion | flops 15032385536 | bytes 40894464 | tf_op jit(solution)/shard_map/dot_general | solution.py:23
Async XLA Ops:
  7.2 78.5 %all-gather.4.cloned.1.call-start = ((), (), s32[]{:S(2)}) async-start(), calls=%async_computation.1 | async-start | bytes 4718592 | tf_op jit(solution)/shard_map/all_gather | solution.py:10
  7.9 208.4 %reduce-scatter.2.cloned.1.call-start = ((), (), s32[]{:S(2)}) async-start(), calls=%async_computation.2 | async-start | bytes 18350080 | tf_op jit(solution)/shard_map/reduce_scatter | solution.py:14
  107.5 169.0 %all-gather.6.cloned.1.call-start = ((), (), s32[]{:S(2)}) async-start(), calls=%async_computation.3 | async-start | bytes 9175040 | tf_op jit(solution)/shard_map/all_gather | solution.py:22
Sparse Core Ops, SparseCore 0:
  10.1 75.4 all-gather.3
  107.6 108.5 reduce-scatter.1
  224.1 52.3 all-gather.5
